TPU v7x, 32 devices: a 4x4x1 block of a 4x4x8 slice. The times are simulated.
32 devices in a mesh: dp: 2 (over z, core), tp: 16 (over x, y).
Axes of the slice: x: 4, y: 4, z: 1, core: 2. Of those that a mesh axis runs over, the one named last changes fastest.
The devices are a block of a 4x4x8 slice.
Arguments:
- x: bfloat16 [4096, 8192], P('dp'), parts along dimension 0
- w_gate: bfloat16 [8192, 28672], P(None, 'tp')
- w_up: bfloat16 [8192, 28672], P(None, 'tp')
- w_down: bfloat16 [28672, 8192], P('tp')
Outputs:
- output: bfloat16 [4096, 8192], P('dp'), parts along dimension 0
There are 2 independent parts. A program takes and returns all parts, laid end to end along the dimension named above; an argument that names none is the same for every part.
All inputs are finite; a program needn't handle non-finite values.
Results may differ from a plain program's by a relative error of at most 0.016.
Values are sent between devices in bfloat16 or wider.
A program may use at most 768 MiB of HBM per device.

v0:
```python
import jax
import jax.numpy as jnp
from jax import lax
from jax.sharding import PartitionSpec as P


def solution(mesh):
    def step(x, w_gate, w_up, w_down):
        gate = jnp.dot(x, w_gate, preferred_element_type=jnp.float32)
        up = jnp.dot(x, w_up, preferred_element_type=jnp.float32)
        hidden = (jax.nn.silu(gate) * up).astype(jnp.bfloat16)
        term = jnp.dot(hidden, w_down, preferred_element_type=jnp.float32).astype(jnp.bfloat16)
        return lax.psum(term, "tp")

    return jax.shard_map(
        step,
        mesh=mesh,
        in_specs=(P("dp", None), P(None, "tp"), P(None, "tp"), P("tp", None)),
        out_specs=P("dp", None),
        check_vma=False,
    )
```

profile of v0, /device:TPU:97, one launch (start us, length us, event | category | flops | bytes accessed | tf_op | source)
XLA Modules:
  0.0 632.7 jit_solution(16877866544088454661)
XLA Ops:
  6.5 0.0 all-reduce.2.cloned.1.call-start
  6.6 69.8 %fusion = f32[2048,1792]{1,0:T(8,128)} fusion(bf16[2048,8192]{1,0:T(8,128)(2,1)} %param.4, bf16[8192,1792]{1,0:T(8,128)(2,1)} %param.5), kind=kOutput, calls=%fused_computation.2 | convolution fusion | flops 60129542144 | bytes 77594624 | tf_op jit(solution)/shard_map/dot_general | solution.py:9
  76.3 74.4 %multiply_convert_fusion = bf16[2048,1792]{1,0:T(8,128)(2,1)} fusion(f32[2048,1792]{1,0:T(8,128)} %fusion, bf16[2048,8192]{1,0:T(8,128)(2,1)} %param.4, bf16[8192,1792]{1,0:T(8,128)(2,1)} %param.6), kind=kOutput, calls=%fused_computation.1 | convolution fusion | flops 60151562240 | bytes 84934656 | tf_op jit(solution)/shard_map/dot_general | solution.py:10
  150.7 68.7 %convolution_convert_fusion = bf16[2048,8192]{1,0:T(8,128)(2,1)} fusion(bf16[2048,1792]{1,0:T(8,128)(2,1)} %multiply_convert_fusion, bf16[1792,8192]{1,0:T(8,128)(2,1)} %param.7), kind=kOutput, calls=%fused_computation | convolution fusion | flops 60146319360 | bytes 70254592 | tf_op jit(solution)/shard_map/dot_general | solution.py:12
  219.4 0.1 all-reduce.2.cloned.1.call-update
  219.5 383.4 %all-reduce.2.cloned.1.call-done = bf16[2048,8192]{1,0:T(8,128)(2,1)} async-done(((bf16[2048,8192]{1,0:T(8,128)(2,1)}), bf16[2048,8192]{1,0:T(8,128)(2,1)}) %all-reduce.2.cloned.1.call-update) | async-done | bytes 33554448 | tf_op jit(solution)/shard_map/psum | solution.py:13
  602.9 23.0 %copy.6 = bf16[2048,8192]{1,0:T(8,128)(2,1)} copy(bf16[2048,8192]{1,0:T(8,128)(2,1)} %all-reduce.2.cloned.1.call-done) | data formatting | bytes 67108864
Async XLA Ops:
  6.5 596.3 %all-reduce.2.cloned.1.call-start = ((), (), s32[]{:S(2)}) async-start(), calls=%async_computation | async-start | bytes 67108864 | tf_op jit(solution)/shard_map/psum | solution.py:13
Sparse Core Ops, SparseCore 0:
  219.6 383.2 all-reduce.1
where the time goes:
time: 633 us
  waiting for transfers between devices  383 us (61%)
  matrix products  213 us (34%)
  local copies, waits for them, and re-layouts  23 us (4%)
  between operations  13.4 us (2%)
    psum x1, waiting for transfers between devices, step(): return lax.psum(term, 'tp')  383 us
    dot_general x1, matrix products, step(): up = jnp.dot(x, w_up, preferred_element_type=jnp.float32)  74.4 us
    dot_general x1, matrix products, step(): gate = jnp.dot(x, w_gate, preferred_element_type=jnp.float32)  69.8 us
    dot_general x1, matrix products, step(): jnp.dot(hidden, w_down, preferred_element_type=jnp.float32)  68.7 us
    unnamed x1, local copies, waits for them, and re-layouts  23 us
  transfers between devices with their start and end apart: 1, of which 1 were waited for; matrix products, arithmetic and copies ran while one was open for 0% of the time, Pallas kernels for 0%

commit v1 on v0

v1 whole, which is shorter than its diff:
```python
import functools
import math

import jax
import jax.numpy as jnp
from jax import lax
from jax.experimental import pallas as pl
from jax.experimental.pallas import tpu as pltpu
from jax.sharding import PartitionSpec as P

CHUNK = 256
TILE = 256
WIDTH = 512
LAG = 3
DEPTH = 8
SENDS = 4
STEPS = 8


def kernel(
    side, x_hbm, wg_hbm, wu_hbm, wd_hbm, y_hbm,
    xbuf, wgu, both, wd, hid, term, part, s1, r1, s2, r2, t1, q1, t2, q2, fin,
    send_sem, recv_sem, x_sem, wgu_sem, wd_sem, own_sem,
):
    rows, d_model = x_hbm.shape
    units = wg_hbm.shape[1]
    chunks = rows // CHUNK
    half = d_model // 2
    per_chunk = half // WIDTH
    tiles = units // TILE
    items = chunks * per_chunk
    big, small = CHUNK // side, CHUNK // side // side
    cut = WIDTH // 2
    me = lax.axis_index("tp")
    pos = (me // side, lax.rem(me, side))

    def near(axis, step):
        at = lax.rem(pos[axis] + step + side, side)
        return at * side + pos[1] if axis == 0 else pos[0] * side + at

    def place(axis, step):
        return lax.rem(pos[axis] + step + side, side)

    barrier = pltpu.get_barrier_semaphore()
    for axis in (0, 1):
        for step in (1, -1):
            pl.semaphore_signal(
                barrier, inc=1, device_id={"tp": near(axis, step)},
                device_id_type=pl.DeviceIdType.MESH,
            )
    pl.semaphore_wait(barrier, 4)

    def copy(k, p, d, item):
        slot, out = lax.rem(item, DEPTH), lax.rem(item, SENDS)
        first, second = p, 1 - p
        axis = (first, first, second, second, second, second, first, first)[k]
        if k == 0:
            src, dst = s1.at[out, p, d], r1.at[slot, p, d]
        elif k == 1:
            src, dst = s2.at[out, p, d], r2.at[slot, p, d]
        elif k == 2:
            src, dst = t1.at[out, p, d], q1.at[slot, p, d]
        elif k == 3:
            src, dst = t2.at[out, p, d], q2.at[slot, p, d]
        else:
            row = lax.div(item, per_chunk) * CHUNK
            col = p * half + lax.rem(item, per_chunk) * WIDTH
            back = -1 if d == 0 else 1
            if k == 4:
                row += pos[first] * big + pos[second] * small
                height, wide = small, WIDTH
            elif k == 5:
                row += pos[first] * big + place(second, back) * small
                height, wide = small, cut
            elif k == 6:
                row += pos[first] * big
                height, wide = big, WIDTH
            else:
                row += place(first, back) * big
                height, wide = big, cut
            if k in (5, 7):
                col += d * cut
            dst = y_hbm.at[
                pl.ds(pl.multiple_of(row, small), height), pl.ds(pl.multiple_of(col, 128), wide)
            ]
            src = fin.at[out, p] if k == 4 else dst
        return pltpu.make_async_remote_copy(
            src_ref=src,
            dst_ref=dst,
            send_sem=send_sem.at[k, p, d, out],
            recv_sem=recv_sem.at[k, p, d, out],
            device_id={"tp": near(axis, 1 if d == 0 else -1)},
            device_id_type=pl.DeviceIdType.MESH,
        )

    def own_copy(p, item):
        out = lax.rem(item, SENDS)
        row = lax.div(item, per_chunk) * CHUNK + pos[p] * big + pos[1 - p] * small
        col = p * half + lax.rem(item, per_chunk) * WIDTH
        return pltpu.make_async_copy(
            fin.at[out, p],
            y_hbm.at[pl.ds(pl.multiple_of(row, small), small), pl.ds(pl.multiple_of(col, 128), WIDTH)],
            own_sem.at[out, p],
        )

    def start_all(k, item):
        for p in (0, 1):
            for d in (0, 1):
                copy(k, p, d, item).start()

    def wait_all(k, item):
        for p in (0, 1):
            for d in (0, 1):
                one = copy(k, p, d, item)
                one.wait_send()
                one.wait_recv()

    low, high = pl.ds(0, cut), pl.ds(cut, cut)

    def block(level, item, p, step, cols):
        slot = lax.rem(item, SENDS)
        if level == 0:
            return term[slot, p, pl.ds(pl.multiple_of(place(p, step) * big, big), big), cols]
        return part[slot, p, pl.ds(pl.multiple_of(place(1 - p, step) * small, small), small), cols]

    def send_first(level, item):
        out = lax.rem(item, SENDS)
        stage = (s1, t1)[level]
        for p in (0, 1):
            stage[out, p, 0, :, low] = block(level, item, p, 2, low).astype(jnp.bfloat16)
            stage[out, p, 0, :, high] = block(level, item, p, 1, high).astype(jnp.bfloat16)
            stage[out, p, 1, :, high] = block(level, item, p, 2, high).astype(jnp.bfloat16)
            stage[out, p, 1, :, low] = block(level, item, p, -1, low).astype(jnp.bfloat16)
        start_all(2 * level, item)

    def send_second(level, item):
        slot, out = lax.rem(item, DEPTH), lax.rem(item, SENDS)
        stage, got = ((s2, r1), (t2, q1))[level]
        wait_all(2 * level, item)
        for p in (0, 1):
            stage[out, p, 0] = (
                block(level, item, p, 1, low) + got[slot, p, 0, :, low].astype(jnp.float32)
            ).astype(jnp.bfloat16)
            stage[out, p, 1] = (
                block(level, item, p, -1, high) + got[slot, p, 1, :, high].astype(jnp.float32)
            ).astype(jnp.bfloat16)
        start_all(2 * level + 1, item)

    def finish(level, item):
        slot, out = lax.rem(item, DEPTH), lax.rem(item, SENDS)
        got1, got2 = ((r1, r2), (q1, q2))[level]
        wait_all(2 * level + 1, item)
        for p in (0, 1):
            left = (
                block(level, item, p, 0, low)
                + got2[slot, p, 0].astype(jnp.float32)
                + got1[slot, p, 1, :, low].astype(jnp.float32)
            )
            right = (
                block(level, item, p, 0, high)
                + got2[slot, p, 1].astype(jnp.float32)
                + got1[slot, p, 0, :, high].astype(jnp.float32)
            )
            if level == 0:
                part[out, p, :, low] = left
                part[out, p, :, high] = right
            else:
                fin[out, p, :, low] = left.astype(jnp.bfloat16)
                fin[out, p, :, high] = right.astype(jnp.bfloat16)

    def step(s, item):
        if s == 1:
            send_second(0, item)
        elif s == 2:
            finish(0, item)
            send_first(1, item)
        elif s == 3:
            send_second(1, item)
        elif s == 4:
            finish(1, item)
            start_all(4, item)
            for p in (0, 1):
                own_copy(p, item).start()
        else:
            wait_all(s - 1, item)
            if s == 5:
                for p in (0, 1):
                    own_copy(p, item).wait()
            if s < STEPS:
                start_all(s, item)

    deep = d_model // 2

    def x_copy(c, h):
        slot = lax.rem(c, 2)
        return pltpu.make_async_copy(
            x_hbm.at[pl.ds(pl.multiple_of(c * CHUNK, CHUNK), CHUNK), pl.ds(h * deep, deep)],
            xbuf.at[slot, :, pl.ds(h * deep, deep)],
            x_sem.at[slot, h],
        )

    def gate_copies(g, h):
        slot = lax.rem(g, 2)
        cols = pl.ds(pl.multiple_of(lax.rem(g, tiles) * TILE, TILE), TILE)
        return [
            pltpu.make_async_copy(
                w.at[pl.ds(h * deep, deep), cols],
                wgu.at[slot, pl.ds(h * deep, deep), pl.ds(n * TILE, TILE)],
                wgu_sem.at[slot, h, n],
            )
            for n, w in enumerate((wg_hbm, wu_hbm))
        ]

    def down_copies(item):
        slot = lax.rem(item, 2)
        return [
            pltpu.make_async_copy(
                wd_hbm.at[:, pl.ds(pl.multiple_of(p * half + lax.rem(item, per_chunk) * WIDTH, WIDTH), WIDTH)],
                wd.at[slot, p],
                wd_sem.at[slot, p],
            )
            for p in (0, 1)
        ]

    def start(copies):
        for one in copies:
            one.start()

    for h in (0, 1):
        x_copy(0, h).start()
        start(gate_copies(0, h))
    for h in (0, 1):
        start(gate_copies(1, h))

    def tick(t, carry):
        c, j = lax.div(t, per_chunk), lax.rem(t, per_chunk)
        item = t - per_chunk
        g = c * tiles + j
        gates = jnp.logical_and(j < tiles, c < chunks)

        def exchange(steps):
            for s in steps:
                older = item - LAG * s // 2

                @pl.when(jnp.logical_and(older >= 0, older < items))
                def _():
                    step(s, older)

        def gate_half(h):
            @pl.when(gates)
            def _():
                @pl.when(j == 0)
                def _():
                    x_copy(c, h).wait()

                for one in gate_copies(g, h):
                    one.wait()
                this = pl.ds(h * deep, deep)
                product = jnp.dot(
                    xbuf[lax.rem(c, 2), :, this], wgu[lax.rem(g, 2), this], preferred_element_type=jnp.float32
                )
                if h == 0:
                    both[...] = product
                else:
                    gate = both[:, :TILE] + product[:, :TILE]
                    up = both[:, TILE:] + product[:, TILE:]
                    hid[lax.rem(c, 2), :, pl.ds(pl.multiple_of(j * TILE, TILE), TILE)] = (
                        jax.nn.silu(gate) * up
                    ).astype(jnp.bfloat16)

                @pl.when(g + 2 < chunks * tiles)
                def _():
                    start(gate_copies(g + 2, h))

        @pl.when(jnp.logical_and(t >= per_chunk - 3, t < per_chunk - 1))
        def _():
            start(down_copies(t - (per_chunk - 3)))

        @pl.when(jnp.logical_and(j == 0, c + 1 < chunks))
        def _():
            for h in (0, 1):
                x_copy(c + 1, h).start()

        exchange(range(STEPS, 0, -2))

        @pl.when(jnp.logical_and(item >= 0, item < items))
        def _():
            for one in down_copies(item):
                one.wait()
            slot = lax.rem(item, SENDS)
            for p in (0, 1):
                term[slot, p] = jnp.dot(
                    hid[lax.rem(c + 1, 2)], wd[lax.rem(item, 2), p], preferred_element_type=jnp.float32
                )
            send_first(0, item)

            @pl.when(item + 2 < items)
            def _():
                start(down_copies(item + 2))

        gate_half(0)
        exchange(range(STEPS - 1, 0, -2))
        gate_half(1)
        return carry

    lax.fori_loop(0, per_chunk + items + LAG * STEPS // 2 + 1, tick, 0)


def solution(mesh):
    side = math.isqrt(mesh.shape["tp"])

    def block_fn(x, w_gate, w_up, w_down):
        d_model, units = w_gate.shape
        big, small, cut = CHUNK // side, CHUNK // side // side, WIDTH // 2
        bf16, f32 = jnp.bfloat16, jnp.float32
        return pl.pallas_call(
            functools.partial(kernel, side),
            out_shape=jax.ShapeDtypeStruct(x.shape, bf16),
            in_specs=[pl.BlockSpec(memory_space=pl.ANY)] * 4,
            out_specs=pl.BlockSpec(memory_space=pl.ANY),
            scratch_shapes=[
                pltpu.VMEM((2, CHUNK, d_model), bf16),
                pltpu.VMEM((2, d_model, 2 * TILE), bf16),
                pltpu.VMEM((CHUNK, 2 * TILE), f32),
                pltpu.VMEM((2, 2, units, WIDTH), bf16),
                pltpu.VMEM((2, CHUNK, units), bf16),
                pltpu.VMEM((SENDS, 2, CHUNK, WIDTH), f32),
                pltpu.VMEM((SENDS, 2, big, WIDTH), f32),
                pltpu.VMEM((SENDS, 2, 2, big, WIDTH), bf16),
                pltpu.VMEM((DEPTH, 2, 2, big, WIDTH), bf16),
                pltpu.VMEM((SENDS, 2, 2, big, cut), bf16),
                pltpu.VMEM((DEPTH, 2, 2, big, cut), bf16),
                pltpu.VMEM((SENDS, 2, 2, small, WIDTH), bf16),
                pltpu.VMEM((DEPTH, 2, 2, small, WIDTH), bf16),
                pltpu.VMEM((SENDS, 2, 2, small, cut), bf16),
                pltpu.VMEM((DEPTH, 2, 2, small, cut), bf16),
                pltpu.VMEM((SENDS, 2, small, WIDTH), bf16),
                pltpu.SemaphoreType.DMA((STEPS, 2, 2, SENDS)),
                pltpu.SemaphoreType.DMA((STEPS, 2, 2, SENDS)),
                pltpu.SemaphoreType.DMA((2, 2)),
                pltpu.SemaphoreType.DMA((2, 2, 2)),
                pltpu.SemaphoreType.DMA((2, 2)),
                pltpu.SemaphoreType.DMA((SENDS, 2)),
            ],
            compiler_params=pltpu.CompilerParams(
                collective_id=0, has_side_effects=True, vmem_limit_bytes=67_043_328
            ),
        )(x, w_gate, w_up, w_down)

    return jax.shard_map(
        block_fn,
        mesh=mesh,
        in_specs=(P("dp", None), P(None, "tp"), P(None, "tp"), P("tp", None)),
        out_specs=P("dp", None),
        check_vma=False,
    )
```

time: 633 us -> 411 us (0.65)
  Pallas kernels: 0 us -> 386 us
  waiting for transfers between devices: 383 us -> 0 us
  matrix products: 213 us -> 0 us
  between operations: 13.4 us -> 0.01 us
    pallas_call x0 -> x1, Pallas kernels: none -> 386 us  [block_fn(): pl.pallas_call(functools.partial(kernel, side), out_shape=jax.ShapeDtypeS...]
    psum x1 -> x0, waiting for transfers between devices: 383 us -> none  [step(): return lax.psum(term, 'tp')]
    dot_general x3 -> x0, matrix products: 213 us -> none  [the longest x1 74.4 us: step(): up = jnp.dot(x, w_up, preferred_element_type=jnp.float32)]
  transfers between devices with their start and end apart: 1 -> 0, of which waited for: 1 -> 0; matrix products, arithmetic and copies ran while one was open for 0% -> 0% of each run, Pallas kernels for 0% -> 0%
where the time goes in v1:
time: 411 us; the launch traced here: 409 us
  Pallas kernels  386 us (94%)
  local copies, waits for them, and re-layouts  23 us (6%)
    pallas_call x1, Pallas kernels, block_fn(): pl.pallas_call(functools.partial(kernel, side), out_shape=jax.ShapeDtypeS...  386 us
    unnamed x1, local copies, waits for them, and re-layouts  23 us

profile of v1, /device:TPU:97, one launch (start us, length us, event | category | flops | bytes accessed | tf_op | source)
XLA Modules:
  0.0 409.5 jit_solution(3073804977969483000)
XLA Ops:
  0.0 386.5 %shard_map.46 = bf16[2048,8192]{1,0:T(8,128)(2,1)} custom-call(bf16[2048,8192]{1,0:T(8,128)(2,1)} %x_hbm.1, bf16[8192,1792]{1,0:T(8,128)(2,1)} %wg_hbm.1, bf16[8192,1792]{1,0:T(8,128)(2,1)} %wu_hbm.1, bf16[1792,8192]{1,0:T(8,128)(2,1)} %wd_hbm.1), custom_call_target="tpu_custom_call" | custom-call | tf_op jit(solution)/shard_map/pallas_call | solution.py:316
  386.5 23.0 %copy.6 = bf16[2048,8192]{1,0:T(8,128)(2,1)} copy(bf16[2048,8192]{1,0:T(8,128)(2,1)} %shard_map.46) | data formatting | bytes 67108864

commit v2 on v1

--- a/solution.py
+++ b/solution.py
@@ -15,6 +15,7 @@
 DEPTH = 8
 SENDS = 4
 STEPS = 8
+LATE = 3
 
 
 def kernel(
@@ -29,6 +30,7 @@
     per_chunk = half // WIDTH
     tiles = units // TILE
     items = chunks * per_chunk
+    early = (chunks - LATE) * per_chunk
     big, small = CHUNK // side, CHUNK // side // side
     cut = WIDTH // 2
     me = lax.axis_index("tp")
@@ -186,8 +188,13 @@
             if s == 5:
                 for p in (0, 1):
                     own_copy(p, item).wait()
-            if s < STEPS:
+            if s < STEPS - 1:
                 start_all(s, item)
+            elif s < STEPS:
+
+                @pl.when(item < early)
+                def _():
+                    start_all(s, item)
 
     deep = d_model // 2
 
@@ -242,7 +249,7 @@
             for s in steps:
                 older = item - LAG * s // 2
 
-                @pl.when(jnp.logical_and(older >= 0, older < items))
+                @pl.when(jnp.logical_and(older >= 0, older < (items if s < STEPS else early)))
                 def _():
                     step(s, older)
 
@@ -303,7 +310,91 @@
         gate_half(1)
         return carry
 
-    lax.fori_loop(0, per_chunk + items + LAG * STEPS // 2 + 1, tick, 0)
+    lax.fori_loop(0, per_chunk + items + LAG * (STEPS - 1) // 2 + 1, tick, 0)
+
+
+def copy_kernel(from_hbm, to_hbm, held, in_sem, out_sem):
+    slots, high, _ = held.shape
+    ahead = slots // 2
+    blocks = from_hbm.shape[0] // high
+
+    def rows(i):
+        return pl.ds(pl.multiple_of(i * high, high), high)
+
+    def read(i):
+        slot = lax.rem(i, slots)
+        return pltpu.make_async_copy(from_hbm.at[rows(i)], held.at[slot], in_sem.at[slot])
+
+    def write(i):
+        slot = lax.rem(i, slots)
+        return pltpu.make_async_copy(held.at[slot], to_hbm.at[rows(i)], out_sem.at[slot])
+
+    for i in range(ahead):
+        read(i).start()
+
+    def move(i, carry):
+        @pl.when(i >= ahead)
+        def _():
+            write(i - ahead).wait()
+
+        @pl.when(i + ahead < blocks)
+        def _():
+            read(i + ahead).start()
+
+        @pl.when(i < blocks)
+        def _():
+            read(i).wait()
+            write(i).start()
+
+        return carry
+
+    lax.fori_loop(0, blocks + ahead, move, 0)
+
+
+def copied(y):
+    rows, d_model = y.shape
+    high, slots = CHUNK // 8, 32
+    return pl.pallas_call(
+        copy_kernel,
+        out_shape=jax.ShapeDtypeStruct(y.shape, y.dtype),
+        in_specs=[pl.BlockSpec(memory_space=pl.ANY)],
+        out_specs=pl.BlockSpec(memory_space=pl.ANY),
+        scratch_shapes=[
+            pltpu.VMEM((slots, high, d_model), y.dtype),
+            pltpu.SemaphoreType.DMA((slots,)),
+            pltpu.SemaphoreType.DMA((slots,)),
+        ],
+        cost_estimate=pl.CostEstimate(
+            flops=600 * y.size, bytes_accessed=4 * y.size, transcendentals=0
+        ),
+    )(y)
+
+
+def last_step(side, y):
+    rows, d_model = y.shape
+    chunks, big, half = rows // CHUNK, CHUNK // side, d_model // 2
+    cut = half // 2
+    me = lax.axis_index("tp")
+    pos = (me // side, lax.rem(me, side))
+    view = y.reshape(chunks, CHUNK, d_model)
+    moved = []
+    for p in (0, 1):
+        for d, step in enumerate((1, -1)):
+            row = lax.rem(pos[p] - step + side, side) * big
+            piece = lax.dynamic_slice(
+                view, (chunks - LATE, row, p * half + d * cut), (LATE, big, cut)
+            )
+            pairs = []
+            for x in range(side):
+                for v in range(side):
+                    to = ((x + step) % side, v) if p == 0 else (x, (v + step) % side)
+                    pairs.append((x * side + v, to[0] * side + to[1]))
+            moved.append((p, d, lax.ppermute(piece, "tp", pairs)))
+    z = copied(y).reshape(chunks, CHUNK, d_model)
+    for p, d, piece in moved:
+        row = lax.rem(pos[p] + 2, side) * big
+        z = lax.dynamic_update_slice(z, piece, (chunks - LATE, row, p * half + d * cut))
+    return z.reshape(rows, d_model)
 
 
 def solution(mesh):
@@ -313,7 +404,7 @@
         d_model, units = w_gate.shape
         big, small, cut = CHUNK // side, CHUNK // side // side, WIDTH // 2
         bf16, f32 = jnp.bfloat16, jnp.float32
-        return pl.pallas_call(
+        y = pl.pallas_call(
             functools.partial(kernel, side),
             out_shape=jax.ShapeDtypeStruct(x.shape, bf16),
             in_specs=[pl.BlockSpec(memory_space=pl.ANY)] * 4,
@@ -346,6 +437,7 @@
                 collective_id=0, has_side_effects=True, vmem_limit_bytes=67_043_328
             ),
         )(x, w_gate, w_up, w_down)
+        return last_step(side, y)
 
     return jax.shard_map(
         block_fn,

time: 411 us -> 406 us (0.988)
  local copies, waits for them, and re-layouts: 23 us -> 7.36 us
  Pallas kernels: 386 us -> 392 us
    unnamed x1 -> x0, local copies, waits for them, and re-layouts: 23 us -> none
    pallas_call x0 -> x1, Pallas kernels: none -> 22.6 us  [copied(): pl.pallas_call(copy_kernel, out_shape=jax.ShapeDtypeStruct(y.shape, y.dty...]
    pallas_call x1, Pallas kernels: 386 us -> 370 us  [block_fn(): pl.pallas_call(functools.partial(kernel, side), out_shape=jax.ShapeDtypeS...]
  transfers between devices with their start and end apart: 0 -> 4, of which waited for: 0 -> 0; matrix products, arithmetic and copies ran while one was open for 0% -> 1% of each run, Pallas kernels for 0% -> 6%
where the time goes in v2:
time: 406 us; the launch traced here: 403 us
  Pallas kernels  392 us (97%)
  local copies, waits for them, and re-layouts  7.36 us (2%)
    pallas_call x1, Pallas kernels, block_fn(): pl.pallas_call(functools.partial(kernel, side), out_shape=jax.ShapeDtypeS...  370 us
    pallas_call x1, Pallas kernels, copied(): pl.pallas_call(copy_kernel, out_shape=jax.ShapeDtypeStruct(y.shape, y.dty...  22.6 us
  transfers between devices with their start and end apart: 4, of which 0 were waited for; matrix products, arithmetic and copies ran while one was open for 1% of the time, Pallas kernels for 6%

profile of v2, /device:TPU:97, one launch (start us, length us, event | category | flops | bytes accessed | tf_op | source)
XLA Modules:
  0.0 402.8 jit_solution(7167988357668822580)
XLA Ops:
  0.0 369.8 %shard_map.46.from_hbm = bf16[2048,8192]{1,0:T(8,128)(2,1)} custom-call(bf16[2048,8192]{1,0:T(8,128)(2,1)} %x_hbm.1, bf16[8192,1792]{1,0:T(8,128)(2,1)} %wg_hbm.1, bf16[8192,1792]{1,0:T(8,128)(2,1)} %wu_hbm.1, bf16[1792,8192]{1,0:T(8,128)(2,1)} %wd_hbm.1), custom_call_target="tpu_custom_call" | custom-call | tf_op jit(solution)/shard_map/pallas_call | solution.py:407
  369.8 3.6 constant_dynamic-slice_fusion
  373.4 1.2 collective-permute-start.3
  374.7 0.3 collective-permute-start.2
  374.9 1.2 collective-permute-start.1
  376.1 0.2 collective-permute-start
  376.4 22.6 %shard_map.47 = bf16[2048,8192]{1,0:T(8,128)(2,1)} custom-call(bf16[2048,8192]{1,0:T(8,128)(2,1)} %shard_map.46.from_hbm), custom_call_target="tpu_custom_call" | custom-call | flops 10066329600 | bytes 67108864 | tf_op jit(solution)/shard_map/pallas_call | solution.py:357
  399.0 0.0 collective-permute-done
  399.0 0.9 constant_dynamic-update-slice_fusion.3
  400.0 0.0 collective-permute-done.1
  400.0 0.9 constant_dynamic-update-slice_fusion.2
  400.9 0.0 collective-permute-done.2
  400.9 0.9 constant_dynamic-update-slice_fusion.1
  401.8 0.0 collective-permute-done.3
  401.8 0.9 constant_dynamic-update-slice_fusion
Async XLA Ops:
  373.4 28.4 %collective-permute-start.3 = (bf16[3,64,2048]{2,1,0:T(8,128)(2,1)}, bf16[3,64,2048]{2,1,0:T(8,128)(2,1)S(1)}, u32[]{:S(2)}, u32[]{:S(2)}) collective-permute-start(bf16[3,64,2048]{2,1,0:T(8,128)(2,1)} %get-tuple-element.5), channel_id=1, source_target_pairs={{0,3},{1,0},{2,1},{3,2},{4,7},{5,4},{6,5},{7,6},{8,11},{9,8},{10,9... | collective-permute-start | bytes 2359304 | tf_op jit(solution)/shard_map/ppermute | solution.py:392
  374.7 26.2 %collective-permute-start.2 = (bf16[3,64,2048]{2,1,0:T(8,128)(2,1)}, bf16[3,64,2048]{2,1,0:T(8,128)(2,1)S(1)}, u32[]{:S(2)}, u32[]{:S(2)}) collective-permute-start(bf16[3,64,2048]{2,1,0:T(8,128)(2,1)} %get-tuple-element.6), channel_id=1, source_target_pairs={{0,1},{1,2},{2,3},{3,0},{4,5},{5,6},{6,7},{7,4},{8,9},{9,10},{10,1... | collective-permute-start | bytes 2359304 | tf_op jit(solution)/shard_map/ppermute | solution.py:392
  374.9 25.1 %collective-permute-start.1 = (bf16[3,64,2048]{2,1,0:T(8,128)(2,1)}, bf16[3,64,2048]{2,1,0:T(8,128)(2,1)S(1)}, u32[]{:S(2)}, u32[]{:S(2)}) collective-permute-start(bf16[3,64,2048]{2,1,0:T(8,128)(2,1)} %get-tuple-element.7), channel_id=1, source_target_pairs={{0,12},{1,13},{2,14},{3,15},{4,0},{5,1},{6,2},{7,3},{8,4},{9,5},{1... | collective-permute-start | bytes 2359304 | tf_op jit(solution)/shard_map/ppermute | solution.py:392
  376.1 22.9 %collective-permute-start = (bf16[3,64,2048]{2,1,0:T(8,128)(2,1)}, bf16[3,64,2048]{2,1,0:T(8,128)(2,1)S(1)}, u32[]{:S(2)}, u32[]{:S(2)}) collective-permute-start(bf16[3,64,2048]{2,1,0:T(8,128)(2,1)} %get-tuple-element.8), channel_id=1, source_target_pairs={{0,4},{1,5},{2,6},{3,7},{4,8},{5,9},{6,10},{7,11},{8,12},{9,13},{1... | collective-permute-start | bytes 2359304 | tf_op jit(solution)/shard_map/ppermute | solution.py:392
